TPU v7x, 32 devices: a whole 2x2x4 slice. The times are simulated.
32 devices in a mesh: member: 2 (over y), gx: 4 (over z), gy: 4 (over x, core).
Axes of the slice: x: 2, y: 2, z: 4, core: 2. Of those that a mesh axis runs over, the one named last changes fastest.
Arguments:
- populations: float32 [19, 32, 64, 128], P(None, ('member', 'gx'), 'gy'), parts along dimension 1, may hold values from 0 to 1, as said below
- heat_level: int32 [32, 64, 128], P(('member', 'gx'), 'gy'), parts along dimension 0, may hold values from 0 to 7
- obstacle: int32 [32, 64, 128], P(('member', 'gx'), 'gy'), parts along dimension 0, may hold values 0 or 1
- heat_table: float32 [8], replicated, may hold values from 0.02 to 0.5
Outputs:
- final_populations: float32 [19, 32, 64, 128], P(None, ('member', 'gx'), 'gy'), parts along dimension 1
- velocity: float32 [3, 32, 64, 128], P(None, ('member', 'gx'), 'gy'), parts along dimension 1
There are 2 independent parts, one for each index of `member`. A program takes and returns all parts, laid end to end along the dimension named above; an argument that names none is the same for every part. Nothing has to cross between parts.
Inputs may be any that keep to these rules, and one draw needn't show every extreme that they name: Positive populations near a local equilibrium, in the direction order of the steps.
All inputs are finite; a program needn't handle non-finite values. No bound on the sum of `obstacle` on one device may be relied on, other than what follows from the above.
Results may differ from a plain program's by a relative error of at most 0.0001.
Values sent between devices are 32-bit elements; how exact they have to be, the bound alone decides.
A program may use at most 64 MiB of HBM per device.

v0:
```python
import jax
import jax.numpy as jnp
import numpy as np
from jax import lax
from jax.sharding import PartitionSpec as P

STEPS = 2


lattice = np.array(
    [
        [0, 0, 0],
        [1, 0, 0],
        [-1, 0, 0],
        [0, 1, 0],
        [0, -1, 0],
        [0, 0, 1],
        [0, 0, -1],
        [1, 1, 0],
        [-1, -1, 0],
        [1, -1, 0],
        [-1, 1, 0],
        [1, 0, 1],
        [-1, 0, -1],
        [1, 0, -1],
        [-1, 0, 1],
        [0, 1, 1],
        [0, -1, -1],
        [0, 1, -1],
        [0, -1, 1],
    ]
)
lattice_weight = [1.0 / 3.0] + [1.0 / 18.0] * 6 + [1.0 / 36.0] * 12
opposite = [0, 2, 1, 4, 3, 6, 5, 8, 7, 10, 9, 12, 11, 14, 13, 16, 15, 18, 17]
base_tau = 0.52
smag_coef = 0.04
speed_cap = 0.1
strain_floor = 1e-06


def extended_2(cells, sides, width, closed):
    for axis, dim in sides:
        count = lax.axis_size(axis)
        ends = count if closed else count - 1
        head = lax.slice_in_dim(cells, 0, width, axis=dim)
        tail = lax.slice_in_dim(cells, cells.shape[dim] - width, cells.shape[dim], axis=dim)
        cells = jnp.concatenate(
            [
                lax.ppermute(tail, axis, [(i, (i + 1) % count) for i in range(ends)]),
                cells,
                lax.ppermute(head, axis, [((i + 1) % count, i) for i in range(ends)]),
            ],
            axis=dim,
        )
    return cells


def stream_all(padded, span_x, span_y, depth_z):
    pieces = []
    for number in range(19):
        shift_x = int(lattice[number][0])
        shift_y = int(lattice[number][1])
        shift_z = int(lattice[number][2])
        pieces.append(
            padded[
                number,
                1 - shift_x : 1 - shift_x + span_x,
                1 - shift_y : 1 - shift_y + span_y,
                1 - shift_z : 1 - shift_z + depth_z,
            ]
        )
    return jnp.stack(pieces)


def moments(read, solid):
    density = jnp.sum(read, axis=0)
    components = []
    for component in range(3):
        moment = jnp.zeros(density.shape, jnp.float32)
        for number in range(19):
            factor = int(lattice[number][component])
            if factor != 0:
                moment = moment + float(factor) * read[number]
        components.append(moment)
    momentum = jnp.stack(components)
    safe_density = jnp.where(solid, 1.0, density)
    velocity = jnp.where(solid[None], 0.0, momentum / safe_density[None])
    return (density, velocity)


def strain_size(vel_wide):
    padded = jnp.pad(vel_wide, ((0, 0), (0, 0), (0, 0), (1, 1)))
    gradient = [
        (padded[:, 2:, 1:-1, 1:-1] - padded[:, :-2, 1:-1, 1:-1]) * 0.5,
        (padded[:, 1:-1, 2:, 1:-1] - padded[:, 1:-1, :-2, 1:-1]) * 0.5,
        (padded[:, 1:-1, 1:-1, 2:] - padded[:, 1:-1, 1:-1, :-2]) * 0.5,
    ]
    strain_sum = jnp.zeros(gradient[0].shape[1:], jnp.float32)
    for row_axis in range(3):
        for col_axis in range(3):
            strain_ab = 0.5 * (gradient[col_axis][row_axis] + gradient[row_axis][col_axis])
            strain_sum = strain_sum + strain_ab * strain_ab
    return jnp.sqrt(2.0 * strain_sum + strain_floor)


def collide(read, density, velocity, solid, magnitude, lift_force):
    relax_time = base_tau + 3.0 * smag_coef * magnitude
    speed_sq = velocity[0] * velocity[0] + velocity[1] * velocity[1] + velocity[2] * velocity[2]
    collided = []
    for number in range(19):
        project = (
            float(lattice[number][0]) * velocity[0]
            + float(lattice[number][1]) * velocity[1]
            + float(lattice[number][2]) * velocity[2]
        )
        equilibrium = (
            lattice_weight[number]
            * density
            * (1.0 + 3.0 * project + 4.5 * project * project - 1.5 * speed_sq)
        )
        fluid_post = (
            read[number]
            - (read[number] - equilibrium) / relax_time
            + 3.0 * lattice_weight[number] * float(lattice[number][2]) * lift_force
        )
        collided.append(jnp.where(solid, read[opposite[number]], fluid_post))
    return jnp.stack(collided)


def lookup(heat_level, heat_table):
    heat_force = jnp.zeros(heat_level.shape, jnp.float32)
    for level_no in range(heat_table.shape[0]):
        heat_force = heat_force + jnp.where(heat_level == level_no, heat_table[level_no], 0.0)
    return heat_force


def wall_flags(anchor_y, total_y, span_x, span_y, depth_z):
    grid_y = anchor_y + lax.broadcasted_iota(jnp.int32, (span_x, span_y, depth_z), 1)
    grid_z = lax.broadcasted_iota(jnp.int32, (span_x, span_y, depth_z), 2)
    return (grid_y <= 0) | (grid_y >= total_y - 1) | (grid_z == 0) | (grid_z == depth_z - 1)


def extend_all(stacked, rim_depth):
    extended = extended_2(stacked, (("gx", 1),), rim_depth, True)
    return extended_2(extended, (("gy", 2),), rim_depth, False)


def local(populations, heat_level, obstacle, heat_table):
    span_x = populations.shape[1]
    span_y = populations.shape[2]
    depth_z = populations.shape[3]
    anchor_y = lax.axis_index("gy") * span_y
    total_y = lax.axis_size("gy") * span_y
    solid_core = (obstacle == 1) | wall_flags(anchor_y, total_y, span_x, span_y, depth_z)
    heat_force = lookup(heat_level, heat_table)
    current = populations
    velocity = jnp.zeros((3, span_x, span_y, depth_z), jnp.float32)
    for repeat in range(STEPS):
        stacked = jnp.concatenate([current, obstacle.astype(jnp.float32)[None]], axis=0)
        extended = extend_all(stacked, 2)
        wide_pops = extended[:19]
        wide_solid = extended[19]
        padded = jnp.pad(wide_pops, ((0, 0), (0, 0), (0, 0), (1, 1)))
        read_wide = stream_all(padded, span_x + 2, span_y + 2, depth_z)
        solid_wide = (wide_solid[1:-1, 1:-1] > 0.5) | wall_flags(
            anchor_y - 1, total_y, span_x + 2, span_y + 2, depth_z
        )
        density_wide, vel_wide = moments(read_wide, solid_wide)
        read = read_wide[:, 1:-1, 1:-1]
        density = density_wide[1:-1, 1:-1]
        velocity = vel_wide[:, 1:-1, 1:-1]
        local_peak = jnp.max(
            velocity[0] * velocity[0] + velocity[1] * velocity[1] + velocity[2] * velocity[2]
        )
        peak_speed = lax.pmax(local_peak, ("gx", "gy"))
        force_scale = speed_cap / jnp.sqrt(speed_cap * speed_cap + peak_speed)
        magnitude = strain_size(vel_wide)
        current = collide(read, density, velocity, solid_core, magnitude, force_scale * heat_force)
    return (current, velocity)


def solution(mesh):
    return jax.shard_map(
        local,
        mesh=mesh,
        in_specs=(
            P(None, ("member", "gx"), "gy", None),
            P(("member", "gx"), "gy", None),
            P(("member", "gx"), "gy", None),
            P(),
        ),
        out_specs=(P(None, ("member", "gx"), "gy", None), P(None, ("member", "gx"), "gy", None)),
        check_vma=False,
    )
```

profile of v0, /device:TPU:0, one launch (start us, length us, event | category | flops | bytes accessed | tf_op | source)
XLA Modules:
  0.0 136.1 jit_solution(301851595374664327)
XLA Ops:
  0.7 0.8 convert_bitcast_fusion
  1.5 1.1 fusion
  2.6 5.1 %collective-permute-start.1 = (f32[20,2,16,128]{3,2,1,0:T(8,128)S(1)}, f32[20,2,16,128]{3,2,1,0:T(8,128)S(1)}, u32[]{:S(2)}, u32[]{:S(2)}) collective-permute-start(f32[20,2,16,128]{3,2,1,0:T(8,128)S(1)} %get-tuple-element.62), channel_id=1, source_target_pairs={{4,0},{8,4},{12,8},{0,12},{5,1},{9,5},{13,9},{1,13},{6,2},{10,6},{... | collective-permute-start | bytes 983048 | tf_op jit(solution)/shard_map/ppermute | solution.py:51
  7.7 0.5 compare_or_fusion.1
  8.3 7.6 %collective-permute-done.1 = f32[20,2,16,128]{3,2,1,0:T(8,128)S(1)} collective-permute-done((f32[20,2,16,128]{3,2,1,0:T(8,128)S(1)}, f32[20,2,16,128]{3,2,1,0:T(8,128)S(1)}, u32[]{:S(2)}, u32[]{:S(2)}) %collective-permute-start.1) | collective-permute-done | bytes 327712 | tf_op jit(solution)/shard_map/ppermute | solution.py:51
  15.8 6.8 %collective-permute-done = f32[20,2,16,128]{3,2,1,0:T(8,128)S(1)} collective-permute-done((f32[20,2,16,128]{3,2,1,0:T(8,128)S(1)}, f32[20,2,16,128]{3,2,1,0:T(8,128)S(1)}, u32[]{:S(2)}, u32[]{:S(2)}) %collective-permute-start) | collective-permute-done | bytes 327712 | tf_op jit(solution)/shard_map/ppermute | solution.py:49
  22.6 1.3 pad_maximum_fusion.9
  23.9 1.3 collective-permute-start.3
  25.2 3.0 %collective-permute-start.2 = (f32[20,8,2,128]{3,2,1,0:T(2,128)S(1)}, f32[20,8,2,128]{3,2,1,0:T(2,128)S(1)}, u32[]{:S(2)}, u32[]{:S(2)}) collective-permute-start(f32[20,8,2,128]{3,2,1,0:T(2,128)S(1)} %get-tuple-element.57), channel_id=1, source_target_pairs={{0,1},{1,2},{2,3},{4,5},{5,6},{6,7},{8,9},{9,10},{10,11},{12,13},{... | collective-permute-start | bytes 491528 | tf_op jit(solution)/shard_map/ppermute | solution.py:49
  28.3 0.7 fusion.454
  29.0 0.3 collective-permute-done.2
  29.3 0.3 pad_maximum_fusion
  29.6 0.1 slice.965
  29.8 0.3 broadcast_select_fusion.1
  30.1 0.3 multiply_add_fusion.3
  30.5 0.2 multiply_add_fusion.2
  30.7 0.7 fusion.450
  31.4 0.8 fusion.10
  32.2 32.8 %pmax.14 = f32[]{:T(128)} all-reduce(f32[]{:T(128)} %get-tuple-element.42), channel_id=1, replica_groups=mesh['member'=2,'gx'=4,'gy'=4] {'gx','gy'}, use_global_device_ids=true, to_apply=%region_1.2 | all-reduce | flops 1 | bytes 8 | tf_op jit(solution)/shard_map/pmax | solution.py:175
  65.6 6.6 %constant_dynamic-update-slice_fusion.19 = (f32[20,4,16,128]{3,2,1,0:T(8,128)S(1)}, f32[4,16,128]{2,1,0:T(8,128)}, f32[4,16,128]{2,1,0:T(8,128)S(1)}, f32[4,16,128]{2,1,0:T(8,128)S(1)}, pred[4,16,128]{2,1,0:T(8,128)(4,1)S(1)}) fusion(f32[]{:T(128)S(6)} %div.139, f32[4,16,128]{2,1,0:T(8,128)S(1)} %get-tuple-element.43, f32[3,6,18,128]{3,2,1,0:T(8,128)S(1)} %fusion.1, ...), kind=kLoop, calls=%fused_computation.94 | loop fusion | flops 638975 | bytes 696628
  72.2 0.8 constant_dynamic-update-slice_fusion.18
  73.1 0.8 constant_dynamic-update-slice_fusion.16
  74.1 0.7 copy-done.2
  74.8 0.1 copy-done.4
  75.6 0.1 constant_dynamic-update-slice_fusion.4
  75.7 0.1 constant_dynamic-update-slice_fusion.3
  75.9 0.1 constant_dynamic-update-slice_fusion.1
  76.0 0.6 copy-done.13
  76.7 2.0 %collective-permute-start.4 = (f32[20,2,16,128]{3,2,1,0:T(8,128)S(1)}, f32[20,2,16,128]{3,2,1,0:T(8,128)S(1)}, u32[]{:S(2)}, u32[]{:S(2)}) collective-permute-start(f32[20,2,16,128]{3,2,1,0:T(8,128)S(1)} %get-tuple-element.59), channel_id=1, source_target_pairs={{0,4},{4,8},{8,12},{12,0},{1,5},{5,9},{9,13},{13,1},{2,6},{6,10},{... | collective-permute-start | bytes 983048 | tf_op jit(solution)/shard_map/ppermute | solution.py:49
  78.7 13.4 %collective-permute-done.5 = f32[20,2,16,128]{3,2,1,0:T(8,128)S(1)} collective-permute-done((f32[20,2,16,128]{3,2,1,0:T(8,128)S(1)}, f32[20,2,16,128]{3,2,1,0:T(8,128)S(1)}, u32[]{:S(2)}, u32[]{:S(2)}) %collective-permute-start.5) | collective-permute-done | bytes 327712 | tf_op jit(solution)/shard_map/ppermute | solution.py:51
  92.1 0.1 pad_maximum_fusion.5
  92.2 1.3 collective-permute-start.7
  93.5 3.0 %collective-permute-start.6 = (f32[20,8,2,128]{3,2,1,0:T(2,128)S(1)}, f32[20,8,2,128]{3,2,1,0:T(2,128)S(1)}, u32[]{:S(2)}, u32[]{:S(2)}) collective-permute-start(f32[20,8,2,128]{3,2,1,0:T(2,128)S(1)} %get-tuple-element.55), channel_id=1, source_target_pairs={{0,1},{1,2},{2,3},{4,5},{5,6},{6,7},{8,9},{9,10},{10,11},{12,13},{... | collective-permute-start | bytes 491528 | tf_op jit(solution)/shard_map/ppermute | solution.py:49
  96.6 1.0 collective-permute-done.6
  97.6 0.3 pad_maximum_fusion.1
  98.0 0.1 slice.986
  98.1 0.5 copy-done.16
  98.6 0.3 broadcast_select_fusion
  98.9 0.3 multiply_add_fusion.1
  99.2 0.2 multiply_add_fusion
  99.4 0.7 fusion.442
  100.1 0.8 fusion.453
  100.9 31.3 %pmax.15 = f32[]{:T(128)} all-reduce(f32[]{:T(128)} %get-tuple-element.16), channel_id=1, replica_groups=mesh['member'=2,'gx'=4,'gy'=4] {'gx','gy'}, use_global_device_ids=true, to_apply=%region_3.4 | all-reduce | flops 1 | bytes 8 | tf_op jit(solution)/shard_map/pmax | solution.py:175
  132.8 1.0 constant_dynamic-update-slice_fusion.38
  134.9 0.1 constant_dynamic-update-slice_fusion.23
  135.0 0.1 constant_dynamic-update-slice_fusion.22
  135.2 0.1 constant_dynamic-update-slice_fusion.20
  135.3 0.8 copy-done.17
  (72 shorter events, 2.4 us)
Async XLA Ops:
  0.6 28.7 %copy-start = (f32[19,4,16,128]{3,2,1,0:T(8,128)S(1)}, f32[19,4,16,128]{3,2,1,0:T(8,128)}, u32[]{:S(2)}) copy-start(f32[19,4,16,128]{3,2,1,0:T(8,128)} %param.4) | copy-start | bytes 1867780
  0.6 27.7 %copy-start.14 = (f32[8]{0:T(128)S(1)}, f32[8]{0:T(128)}, u32[]{:S(2)}) copy-start(f32[8]{0:T(128)} %param.7) | copy-start | bytes 100
  2.6 13.2 %collective-permute-start.1 = (f32[20,2,16,128]{3,2,1,0:T(8,128)S(1)}, f32[20,2,16,128]{3,2,1,0:T(8,128)S(1)}, u32[]{:S(2)}, u32[]{:S(2)}) collective-permute-start(f32[20,2,16,128]{3,2,1,0:T(8,128)S(1)} %get-tuple-element.62), channel_id=1, source_target_pairs={{4,0},{8,4},{12,8},{0,12},{5,1},{9,5},{13,9},{1,13},{6,2},{10,6},{... | collective-permute-start | bytes 983048 | tf_op jit(solution)/shard_map/ppermute | solution.py:51
  7.7 14.9 %collective-permute-start = (f32[20,2,16,128]{3,2,1,0:T(8,128)S(1)}, f32[20,2,16,128]{3,2,1,0:T(8,128)S(1)}, u32[]{:S(2)}, u32[]{:S(2)}) collective-permute-start(f32[20,2,16,128]{3,2,1,0:T(8,128)S(1)} %get-tuple-element.61), channel_id=1, source_target_pairs={{0,4},{4,8},{8,12},{12,0},{1,5},{5,9},{9,13},{13,1},{2,6},{6,10},{... | collective-permute-start | bytes 983048 | tf_op jit(solution)/shard_map/ppermute | solution.py:49
  15.8 14.6 %copy-start.1 = (f32[20,2,16,128]{3,2,1,0:T(8,128)}, f32[20,2,16,128]{3,2,1,0:T(8,128)S(1)}, u32[]{:S(2)}) copy-start(f32[20,2,16,128]{3,2,1,0:T(8,128)S(1)} %collective-permute-done.1) | copy-start | bytes 983044
  22.6 7.8 %copy-start.3 = (f32[20,2,16,128]{3,2,1,0:T(8,128)}, f32[20,2,16,128]{3,2,1,0:T(8,128)S(1)}, u32[]{:S(2)}) copy-start(f32[20,2,16,128]{3,2,1,0:T(8,128)S(1)} %collective-permute-done) | copy-start | bytes 983044
  23.9 5.1 %collective-permute-start.3 = (f32[20,8,2,128]{3,2,1,0:T(2,128)S(1)}, f32[20,8,2,128]{3,2,1,0:T(2,128)S(1)}, u32[]{:S(2)}, u32[]{:S(2)}) collective-permute-start(f32[20,8,2,128]{3,2,1,0:T(2,128)S(1)} %get-tuple-element.58), channel_id=1, source_target_pairs={{1,0},{2,1},{3,2},{5,4},{6,5},{7,6},{9,8},{10,9},{11,10},{13,12},{... | collective-permute-start | bytes 491528 | tf_op jit(solution)/shard_map/ppermute | solution.py:51
  25.2 4.0 %collective-permute-start.2 = (f32[20,8,2,128]{3,2,1,0:T(2,128)S(1)}, f32[20,8,2,128]{3,2,1,0:T(2,128)S(1)}, u32[]{:S(2)}, u32[]{:S(2)}) collective-permute-start(f32[20,8,2,128]{3,2,1,0:T(2,128)S(1)} %get-tuple-element.57), channel_id=1, source_target_pairs={{0,1},{1,2},{2,3},{4,5},{5,6},{6,7},{8,9},{9,10},{10,11},{12,13},{... | collective-permute-start | bytes 491528 | tf_op jit(solution)/shard_map/ppermute | solution.py:49
  28.3 1.5 %copy-start.15 = (pred[18]{0:T(512)(128)(4,1)}, pred[18]{0:T(512)(128)(4,1)S(1)}, u32[]{:S(2)}) copy-start(pred[18]{0:T(512)(128)(4,1)S(1)} %compare_or_fusion) | copy-start | bytes 58
  29.0 1.5 %copy-start.5 = (f32[20,8,2,128]{3,2,1,0:T(2,128)}, f32[20,8,2,128]{3,2,1,0:T(2,128)S(1)}, u32[]{:S(2)}) copy-start(f32[20,8,2,128]{3,2,1,0:T(2,128)S(1)} %collective-permute-done.3) | copy-start | bytes 491524
  29.3 1.2 copy-start.7
  73.9 1.0 copy-start.2
  73.9 1.1 copy-start.4
  73.9 1.1 copy-start.6
  73.9 1.1 copy-start.8
  75.8 0.8 copy-start.13
  76.6 15.5 %collective-permute-start.5 = (f32[20,2,16,128]{3,2,1,0:T(8,128)S(1)}, f32[20,2,16,128]{3,2,1,0:T(8,128)S(1)}, u32[]{:S(2)}, u32[]{:S(2)}) collective-permute-start(f32[20,2,16,128]{3,2,1,0:T(8,128)S(1)} %get-tuple-element.60), channel_id=1, source_target_pairs={{4,0},{8,4},{12,8},{0,12},{5,1},{9,5},{13,9},{1,13},{6,2},{10,6},{... | collective-permute-start | bytes 983048 | tf_op jit(solution)/shard_map/ppermute | solution.py:51
  76.7 15.4 %collective-permute-start.4 = (f32[20,2,16,128]{3,2,1,0:T(8,128)S(1)}, f32[20,2,16,128]{3,2,1,0:T(8,128)S(1)}, u32[]{:S(2)}, u32[]{:S(2)}) collective-permute-start(f32[20,2,16,128]{3,2,1,0:T(8,128)S(1)} %get-tuple-element.59), channel_id=1, source_target_pairs={{0,4},{4,8},{8,12},{12,0},{1,5},{5,9},{9,13},{13,1},{2,6},{6,10},{... | collective-permute-start | bytes 983048 | tf_op jit(solution)/shard_map/ppermute | solution.py:49
  92.2 4.4 %collective-permute-start.7 = (f32[20,8,2,128]{3,2,1,0:T(2,128)S(1)}, f32[20,8,2,128]{3,2,1,0:T(2,128)S(1)}, u32[]{:S(2)}, u32[]{:S(2)}) collective-permute-start(f32[20,8,2,128]{3,2,1,0:T(2,128)S(1)} %get-tuple-element.56), channel_id=1, source_target_pairs={{1,0},{2,1},{3,2},{5,4},{6,5},{7,6},{9,8},{10,9},{11,10},{13,12},{... | collective-permute-start | bytes 491528 | tf_op jit(solution)/shard_map/ppermute | solution.py:51
  93.5 4.0 %collective-permute-start.6 = (f32[20,8,2,128]{3,2,1,0:T(2,128)S(1)}, f32[20,8,2,128]{3,2,1,0:T(2,128)S(1)}, u32[]{:S(2)}, u32[]{:S(2)}) collective-permute-start(f32[20,8,2,128]{3,2,1,0:T(2,128)S(1)} %get-tuple-element.55), channel_id=1, source_target_pairs={{0,1},{1,2},{2,3},{4,5},{5,6},{6,7},{8,9},{9,10},{10,11},{12,13},{... | collective-permute-start | bytes 491528 | tf_op jit(solution)/shard_map/ppermute | solution.py:49
  96.6 2.6 %copy-start.9 = (f32[20,8,2,128]{3,2,1,0:T(2,128)}, f32[20,8,2,128]{3,2,1,0:T(2,128)S(1)}, u32[]{:S(2)}) copy-start(f32[20,8,2,128]{3,2,1,0:T(2,128)S(1)} %collective-permute-done.7) | copy-start | bytes 491524
  97.6 1.6 %copy-start.11 = (f32[20,8,2,128]{3,2,1,0:T(2,128)}, f32[20,8,2,128]{3,2,1,0:T(2,128)S(1)}, u32[]{:S(2)}) copy-start(f32[20,8,2,128]{3,2,1,0:T(2,128)S(1)} %collective-permute-done.6) | copy-start | bytes 491524
  97.9 0.6 copy-start.16
  132.8 1.2 copy-start.10
  132.8 1.2 copy-start.12
  135.3 0.8 copy-start.17
where the time goes:
time: 137 us; the launch traced here: 136 us
  blocking collectives  64.1 us (47%)
  waiting for transfers between devices  29 us (21%)
  other arithmetic  20.9 us (15%)
  starting transfers between devices  15.9 us (12%)
  local copies, waits for them, and re-layouts  3.82 us (3%)
  between operations  2.37 us (2%)
    pmax x2, blocking collectives, local(): peak_speed = lax.pmax(local_peak, ('gx', 'gy'))  64.1 us
    ppermute x4, waiting for transfers between devices, extended_2(): lax.ppermute(head, axis, [((i + 1) % count, i) for i in range(ends)])  21 us
    unnamed x37, other arithmetic  11.6 us
    ppermute x4, starting transfers between devices, extended_2(): lax.ppermute(tail, axis, [(i, (i + 1) % count) for i in range(ends)])  8.1 us
    ppermute x4, waiting for transfers between devices, extended_2(): lax.ppermute(tail, axis, [(i, (i + 1) % count) for i in range(ends)])  8.05 us
    ppermute x4, starting transfers between devices, extended_2(): lax.ppermute(head, axis, [((i + 1) % count, i) for i in range(ends)])  7.77 us
    unnamed x36, local copies, waits for them, and re-layouts  2.84 us
  transfers between devices with their start and end apart: 8, of which 5 were waited for; matrix products, arithmetic and copies ran while one was open for 1% of the time, Pallas kernels for 0%

commit v1 on v0

v1 whole, which is shorter than its diff:
```python
import functools

import jax
import jax.numpy as jnp
import numpy as np
from jax import lax
from jax.experimental import pallas as pl
from jax.experimental.pallas import tpu as pltpu
from jax.sharding import PartitionSpec as P

STEPS = 2
ROW = 8

lattice = np.array(
    [
        [0, 0, 0],
        [1, 0, 0],
        [-1, 0, 0],
        [0, 1, 0],
        [0, -1, 0],
        [0, 0, 1],
        [0, 0, -1],
        [1, 1, 0],
        [-1, -1, 0],
        [1, -1, 0],
        [-1, 1, 0],
        [1, 0, 1],
        [-1, 0, -1],
        [1, 0, -1],
        [-1, 0, 1],
        [0, 1, 1],
        [0, -1, -1],
        [0, 1, -1],
        [0, -1, 1],
    ]
)
CS = [tuple(int(c) for c in row) for row in lattice]
WEIGHT = [1.0 / 3.0] + [1.0 / 18.0] * 6 + [1.0 / 36.0] * 12
OPP = [0, 2, 1, 4, 3, 6, 5, 8, 7, 10, 9, 12, 11, 14, 13, 16, 15, 18, 17]
base_tau = 0.52
smag_coef = 0.04
speed_cap = 0.1
strain_floor = 1e-06
LIFTED = [k for k in range(19) if CS[k][2] != 0]
FLAT = [k for k in range(19) if CS[k][2] == 0]


def tree_sum(items):
    items = list(items)
    while len(items) > 1:
        items = [items[i] + items[i + 1] if i + 1 < len(items) else items[i] for i in range(0, len(items), 2)]
    return items[0]


def kernel(
    ngx, ngy,
    pops, heat_level, obstacle, table,
    out_p, out_v,
    st0, st1, rd, rho_s, v0, v1, hl, ob, solid_s, obuf, pm_src, pm_gy, pm_gx,
    load_sem, a_send, a_recv, b_send, b_recv, p_send, p_recv, out_sem,
):
    _, sx, sy, nz = pops.shape
    levels = table.shape[0]
    gx = lax.axis_index("gx")
    gy = lax.axis_index("gy")
    has_up = gy < ngy - 1
    has_down = gy > 0
    right = lax.rem(gx + 1, ngx)
    left = lax.rem(gx + ngx - 1, ngx)
    own_x = pl.ds(1, sx)
    own_y = pl.ds(ROW, sy)
    top = pl.ds(ROW + sy - 1, 1)
    bottom = pl.ds(ROW, 1)
    rim_low = pl.ds(ROW - 1, 1)
    rim_high = pl.ds(ROW + sy, 1)

    load_p = pltpu.make_async_copy(pops, st0.at[:, own_x, own_y, :], load_sem.at[0])
    load_h = pltpu.make_async_copy(heat_level, hl, load_sem.at[1])
    load_o = pltpu.make_async_copy(obstacle, ob, load_sem.at[2])
    load_p.start()
    load_h.start()
    load_o.start()

    barrier = pltpu.get_barrier_semaphore()

    def greet(x, y):
        pl.semaphore_signal(barrier, inc=1, device_id={"gx": x, "gy": y}, device_id_type=pl.DeviceIdType.MESH)

    for d in range(1, ngx):
        greet(lax.rem(gx + d, ngx), gy)
    for d in range(1, ngy):
        greet(gx, lax.rem(gy + d, ngy))

    @pl.when(has_up)
    def _():
        greet(right, gy + 1)
        greet(left, gy + 1)

    @pl.when(has_down)
    def _():
        greet(right, gy - 1)
        greet(left, gy - 1)

    def zero_rim(rows):
        for ref in (st0, st1, v0, v1):
            ref[:, :, rows, :] = jnp.zeros((ref.shape[0], sx + 2, 1, nz), jnp.float32)

    @pl.when(jnp.logical_not(has_down))
    def _():
        zero_rim(rim_low)

    @pl.when(jnp.logical_not(has_up))
    def _():
        zero_rim(rim_high)

    sides = (
        (None, right, gy, (1, 0)),
        (None, left, gy, (-1, 0)),
        (has_up, gx, gy + 1, (0, 1)),
        (has_down, gx, gy - 1, (0, -1)),
        (has_up, right, gy + 1, (1, 1)),
        (has_down, left, gy - 1, (-1, -1)),
        (has_down, right, gy - 1, (1, -1)),
        (has_up, left, gy + 1, (-1, 1)),
    )
    arrives = (None, None, has_down, has_up, has_down, has_up, has_up, has_down)

    def src_dst(direction):
        dx, dy = direction
        xs = {1: (sx, 0), -1: (1, sx + 1), 0: (own_x, own_x)}[dx]
        ys = {1: (top, rim_low), -1: (bottom, rim_high), 0: (own_y, own_y)}[dy]
        return (xs[0], ys[0]), (xs[1], ys[1])

    def guarded(cond, fn):
        if cond is None:
            fn()
        else:
            pl.when(cond)(fn)

    def moving(direction):
        dx, dy = direction
        if dx and dy:
            return [k for k in range(19) if CS[k][:2] == direction]
        return [k for k in range(19) if (CS[k][0] == dx if dx else CS[k][1] == dy)]

    def exchange(ref, send, recv, many, groups):
        def start(number, x, y, direction):
            def go():
                s, d = src_dst(direction)
                for g in groups(direction):
                    pltpu.make_async_remote_copy(
                        src_ref=ref.at[g, s[0], s[1], :],
                        dst_ref=ref.at[g, d[0], d[1], :],
                        send_sem=send.at[number],
                        recv_sem=recv.at[number],
                        device_id={"gx": x, "gy": y},
                        device_id_type=pl.DeviceIdType.MESH,
                    ).start()
            return go

        for number, (cond, x, y, direction) in enumerate(sides[:many]):
            guarded(cond, start(number, x, y, direction))

        def total(number, direction, sem):
            def go():
                s, _ = src_dst(direction)
                gs = groups(direction)
                view = ref.at[pl.ds(0, len(gs)) if isinstance(gs[0], int) else gs[0], s[0], s[1], :]
                pltpu.make_async_copy(view, view, sem.at[number]).wait()
            return go

        def wait_recv():
            for number in range(many):
                guarded(arrives[number], total(number, sides[number][3], recv))

        def wait_send():
            for number in range(many):
                guarded(sides[number][0], total(number, sides[number][3], send))

        return wait_recv, wait_send

    def spread(step, phase, value, buf):
        count = buf.shape[1]
        pm_src[step, phase] = value
        for d in range(1, count + 1):
            place = {"gy": lax.rem(gy + d, ngy)} if phase == 0 else {"gx": lax.rem(gx + d, ngx)}
            pltpu.make_async_remote_copy(
                src_ref=pm_src.at[step, phase],
                dst_ref=buf.at[step, d - 1],
                send_sem=p_send.at[step, phase],
                recv_sem=p_recv.at[step, phase],
                device_id=place,
                device_id_type=pl.DeviceIdType.MESH,
            ).start()

        def wait():
            pltpu.make_async_copy(buf.at[step], buf.at[step], p_recv.at[step, phase]).wait()
            best = value
            for d in range(count):
                best = jnp.maximum(best, buf[step, d])
            return best

        def wait_send():
            pltpu.make_async_copy(buf.at[step], buf.at[step], p_send.at[step, phase]).wait()

        return wait, wait_send

    blocks = [(x, r) for x in range(sx) for r in range(0, sy, ROW)]
    lane = lax.broadcasted_iota(jnp.int32, (ROW, nz), 1)
    first_lane = lane == 0
    last_lane = lane == nz - 1

    def streamed(st, fs):
        peak = jnp.zeros((ROW, nz), jnp.float32)
        vel = v0 if st is st0 else v1
        for x, r in blocks:
            reads = []
            for k, (cx, cy, cz) in enumerate(CS):
                rows = pl.ds(ROW + r - cy, ROW)
                cells = st[k, x + 1 - cx, rows, :]
                if cz:
                    if fs is not None:
                        cells = cells + (3.0 * WEIGHT[k] * cz) * (fs * v0[3, x + 1 - cx, rows, :])
                    cells = pltpu.roll(cells, cz % nz, 1)
                    cells = jnp.where(first_lane if cz > 0 else last_lane, 0.0, cells)
                rd[k, x, pl.ds(r, ROW), :] = cells
                reads.append(cells)
            density = tree_sum(reads)
            solid = solid_s[x, pl.ds(r, ROW), :] != 0
            inv = jnp.where(solid, 0.0, 1.0 / jnp.where(solid, 1.0, density))
            rho_s[x, pl.ds(r, ROW), :] = density
            speed = []
            for c in range(3):
                plus = tree_sum([reads[k] for k in range(19) if CS[k][c] > 0])
                minus = tree_sum([reads[k] for k in range(19) if CS[k][c] < 0])
                u = (plus - minus) * inv
                vel[c, x + 1, pl.ds(ROW + r, ROW), :] = u
                speed.append(u * u)
            peak = jnp.maximum(peak, speed[0] + speed[1] + speed[2])
        return peak

    def collided(vel, store):
        for x, r in blocks:
            mid = pl.ds(ROW + r, ROW)
            u = [vel[c, x + 1, mid, :] for c in range(3)]
            diff = []
            for a in range(3):
                diff.append(
                    (
                        vel[a, x + 2, mid, :] - vel[a, x, mid, :],
                        vel[a, x + 1, pl.ds(ROW + r + 1, ROW), :] - vel[a, x + 1, pl.ds(ROW + r - 1, ROW), :],
                        pltpu.roll(u[a], nz - 1, 1) - pltpu.roll(u[a], 1, 1),
                    )
                )
            own = diff[0][0] * diff[0][0] + diff[1][1] * diff[1][1] + diff[2][2] * diff[2][2]
            xy = diff[0][1] + diff[1][0]
            xz = diff[0][2] + diff[2][0]
            yz = diff[1][2] + diff[2][1]
            size = jnp.sqrt(0.5 * own + 0.25 * (xy * xy + xz * xz + yz * yz) + strain_floor)
            omega = 1.0 / (base_tau + 3.0 * smag_coef * size)
            solid = solid_s[x, pl.ds(r, ROW), :] != 0
            density = rho_s[x, pl.ds(r, ROW), :]
            still = 1.0 - 1.5 * (u[0] * u[0] + u[1] * u[1] + u[2] * u[2])
            reads = [rd[k, x, pl.ds(r, ROW), :] for k in range(19)]
            scaled = {w: (w * density) * omega for w in sorted(set(WEIGHT))}
            keep = 1.0 - omega
            store(0, x, r, jnp.where(solid, reads[0], keep * reads[0] + scaled[WEIGHT[0]] * still))
            for k in range(1, 19, 2):
                other = OPP[k]
                project = None
                for c in range(3):
                    if CS[k][c]:
                        if project is None:
                            project = u[c] if CS[k][c] > 0 else -u[c]
                        else:
                            project = project + u[c] if CS[k][c] > 0 else project - u[c]
                even = still + 4.5 * project * project
                odd = 3.0 * project
                weight = scaled[WEIGHT[k]]
                store(k, x, r, jnp.where(solid, reads[other], keep * reads[k] + weight * (even + odd)))
                store(other, x, r, jnp.where(solid, reads[k], keep * reads[other] + weight * (even - odd)))

    def scale_of(tile):
        peak = jnp.max(jnp.max(tile, axis=0, keepdims=True), axis=1, keepdims=True)
        peak = jnp.broadcast_to(peak, (ROW, nz))
        return speed_cap / jnp.sqrt(speed_cap * speed_cap + peak)

    gone = []

    partners = (ngx - 1) + (ngy - 1) + 2 * (jnp.where(has_up, 1, 0) + jnp.where(has_down, 1, 0))
    load_p.wait()
    pl.semaphore_wait(barrier, partners)
    wait_a, sent = exchange(st0, a_send.at[0], a_recv.at[0], 8, moving)
    gone.append(sent)
    load_h.wait()
    load_o.wait()
    for x, r in blocks:
        rows = pl.ds(r, ROW)
        code = hl[x, rows, :]
        heat = jnp.zeros((ROW, nz), jnp.float32)
        for level in range(levels):
            heat = jnp.where(code == level, table[level], heat)
        grid_y = gy * sy + r + lax.broadcasted_iota(jnp.int32, (ROW, nz), 0)
        solid = (
            (ob[x, rows, :] == 1) | (grid_y == 0) | (grid_y == ngy * sy - 1) | first_lane | last_lane
        )
        solid_s[x, rows, :] = jnp.where(solid, 1, 0)
        v0[3, x + 1, pl.ds(ROW + r, ROW), :] = jnp.where(solid, 0.0, heat)
    wait_a()
    peak = streamed(st0, None)

    wait_b, sent = exchange(v0, b_send.at[0], b_recv.at[0], 4, lambda direction: [pl.ds(0, 4)])
    gone.append(sent)
    wait_y, sent = spread(0, 0, peak, pm_gy)
    gone.append(sent)
    wait_b()
    wait_x, sent = spread(0, 1, wait_y(), pm_gx)
    gone.append(sent)

    def store_st1(k, x, r, value):
        st1[k, x + 1, pl.ds(ROW + r, ROW), :] = value

    collided(v0, store_st1)

    wait_a, sent = exchange(st1, a_send.at[1], a_recv.at[1], 8, moving)
    gone.append(sent)
    fs = scale_of(wait_x())
    wait_a()
    peak = streamed(st1, fs)

    wait_b, sent = exchange(v1, b_send.at[1], b_recv.at[1], 4, lambda direction: [pl.ds(0, 3)])
    gone.append(sent)
    wait_y, sent = spread(1, 0, peak, pm_gy)
    gone.append(sent)
    send_v = pltpu.make_async_copy(v1.at[:, own_x, own_y, :], out_v, out_sem.at[19])
    send_v.start()
    wait_b()
    wait_x, sent = spread(1, 1, wait_y(), pm_gx)
    gone.append(sent)

    def store_out(k, x, r, value):
        obuf[k, x, pl.ds(r, ROW), :] = value

    collided(v1, store_out)
    outs = {k: pltpu.make_async_copy(obuf.at[k], out_p.at[k], out_sem.at[k]) for k in range(19)}
    for k in FLAT:
        outs[k].start()
    fs = scale_of(wait_x())
    lift = {(x, r): fs * v0[3, x + 1, pl.ds(ROW + r, ROW), :] for x, r in blocks}
    for k in LIFTED:
        for x, r in blocks:
            rows = pl.ds(r, ROW)
            obuf[k, x, rows, :] = obuf[k, x, rows, :] + (3.0 * WEIGHT[k] * CS[k][2]) * lift[(x, r)]
        outs[k].start()
    for sent in gone:
        sent()
    send_v.wait()
    for k in range(19):
        outs[k].wait()


def local(populations, heat_level, obstacle, heat_table):
    ngx = lax.axis_size("gx")
    ngy = lax.axis_size("gy")
    _, sx, sy, nz = populations.shape
    f32 = jnp.float32
    wide = (sx + 2, sy + 2 * ROW, nz)
    dma = pltpu.SemaphoreType.DMA
    return pl.pallas_call(
        functools.partial(kernel, ngx, ngy),
        out_shape=(
            jax.ShapeDtypeStruct(populations.shape, f32),
            jax.ShapeDtypeStruct((3, sx, sy, nz), f32),
        ),
        in_specs=[pl.BlockSpec(memory_space=pl.ANY)] * 3 + [pl.BlockSpec(memory_space=pltpu.SMEM)],
        out_specs=[pl.BlockSpec(memory_space=pl.ANY)] * 2,
        scratch_shapes=[
            pltpu.VMEM((19,) + wide, f32),
            pltpu.VMEM((19,) + wide, f32),
            pltpu.VMEM((19, sx, sy, nz), f32),
            pltpu.VMEM((sx, sy, nz), f32),
            pltpu.VMEM((4,) + wide, f32),
            pltpu.VMEM((3,) + wide, f32),
            pltpu.VMEM((sx, sy, nz), jnp.int32),
            pltpu.VMEM((sx, sy, nz), jnp.int32),
            pltpu.VMEM((sx, sy, nz), jnp.int32),
            pltpu.VMEM((19, sx, sy, nz), f32),
            pltpu.VMEM((STEPS, 2, ROW, nz), f32),
            pltpu.VMEM((STEPS, ngy - 1, ROW, nz), f32),
            pltpu.VMEM((STEPS, ngx - 1, ROW, nz), f32),
            dma((3,)),
            dma((STEPS, 8)),
            dma((STEPS, 8)),
            dma((STEPS, 4)),
            dma((STEPS, 4)),
            dma((STEPS, 2)),
            dma((STEPS, 2)),
            dma((20,)),
        ],
        compiler_params=pltpu.CompilerParams(collective_id=0, has_side_effects=True),
        name="lattice_steps",
    )(populations, heat_level, obstacle, heat_table)


def solution(mesh):
    return jax.shard_map(
        local,
        mesh=mesh,
        in_specs=(
            P(None, ("member", "gx"), "gy", None),
            P(("member", "gx"), "gy", None),
            P(("member", "gx"), "gy", None),
            P(),
        ),
        out_specs=(P(None, ("member", "gx"), "gy", None), P(None, ("member", "gx"), "gy", None)),
        check_vma=False,
    )
```

time: 137 us -> 31.7 us (0.23)
  blocking collectives: 64.1 us -> 0 us
  waiting for transfers between devices: 29 us -> 0 us
  Pallas kernels: 0 us -> 28.3 us
  other arithmetic: 20.9 us -> 0 us
  starting transfers between devices: 15.9 us -> 0 us
  between operations: 2.37 us -> 0.65 us
    pmax x2 -> x0, blocking collectives: 64.1 us -> none  [local(): peak_speed = lax.pmax(local_peak, ('gx', 'gy'))]
    ppermute x8 -> x0, waiting for transfers between devices: 29 us -> none  [the longest x4 21 us: extended_2(): lax.ppermute(head, axis, [((i + 1) % count, i) for i in range(ends)])]
    pallas_call x0 -> x1, Pallas kernels: none -> 28.3 us  [local(): pl.pallas_call(functools.partial(kernel, ngx, ngy), out_shape=(jax.ShapeD...]
    ppermute x8 -> x0, starting transfers between devices: 15.9 us -> none  [the longest x4 8.1 us: extended_2(): lax.ppermute(tail, axis, [(i, (i + 1) % count) for i in range(ends)])]
    unnamed x37 -> x0, other arithmetic: 11.6 us -> none
    slice x3 -> x0, other arithmetic: 2.21 us -> none  [the longest x2 1.43 us: extended_2(): lax.slice_in_dim(cells, cells.shape[dim] - width, cells.shape[dim], axis=...]
    concatenate x4 -> x0, other arithmetic: 1.8 us -> none  [the longest x2 1.12 us: local(): jnp.concatenate([current, obstacle.astype(jnp.float32)[None]], axis=0)]
    unnamed x36 -> x4, local copies, waits for them, and re-layouts: 2.84 us -> 2.63 us
  transfers between devices with their start and end apart: 8 -> 0, of which waited for: 5 -> 0; matrix products, arithmetic and copies ran while one was open for 1% -> 0% of each run, Pallas kernels for 0% -> 0%
where the time goes in v1:
time: 31.7 us; the launch traced here: 31.6 us
  Pallas kernels  28.3 us (89%)
  local copies, waits for them, and re-layouts  2.63 us (8%)
  between operations  0.65 us (2%)
    pallas_call x1, Pallas kernels, local(): pl.pallas_call(functools.partial(kernel, ngx, ngy), out_shape=(jax.ShapeD...  28.3 us
    unnamed x4, local copies, waits for them, and re-layouts  2.63 us

profile of v1, /device:TPU:0, one launch (start us, length us, event | category | flops | bytes accessed | tf_op | source)
XLA Modules:
  0.0 31.6 jit_solution(6481383976995924877)
XLA Ops:
  0.6 28.3 %lattice_steps.1 = (f32[19,4,16,128]{3,2,1,0:T(8,128)}, f32[3,4,16,128]{3,2,1,0:T(8,128)}) custom-call(f32[19,4,16,128]{3,2,1,0:T(8,128)} %pops.1, s32[4,16,128]{2,1,0:T(8,128)} %heat_level.1, s32[4,16,128]{2,1,0:T(8,128)} %obstacle.1, f32[8]{0:T(128)} %table.1), custom_call_target="tpu_custom_call" | custom-call | tf_op jit(solution)/shard_map/lattice_steps/pallas_call | solution.py:369
  28.9 0.0 copy-start
  28.9 2.0 %copy.8 = f32[19,4,16,128]{3,2,1,0:T(8,128)} copy(f32[19,4,16,128]{3,2,1,0:T(8,128)} %get-tuple-element.4) | data formatting | bytes 1245184
  30.9 0.0 copy-done
  30.9 0.6 %copy.9 = f32[3,4,16,128]{3,2,1,0:T(8,128)} copy(f32[3,4,16,128]{3,2,1,0:T(8,128)S(1)} %copy-done) | data formatting | bytes 196608
Async XLA Ops:
  28.9 2.0 %copy-start = (f32[3,4,16,128]{3,2,1,0:T(8,128)S(1)}, f32[3,4,16,128]{3,2,1,0:T(8,128)}, u32[]{:S(2)}) copy-start(f32[3,4,16,128]{3,2,1,0:T(8,128)} %get-tuple-element.5) | copy-start | bytes 294916

commit v2 on v1

--- a/solution.py
+++ b/solution.py
@@ -42,7 +42,6 @@
 speed_cap = 0.1
 strain_floor = 1e-06
 LIFTED = [k for k in range(19) if CS[k][2] != 0]
-FLAT = [k for k in range(19) if CS[k][2] == 0]
 
 
 def tree_sum(items):
@@ -52,13 +51,19 @@
     return items[0]
 
 
+def peak_groups(ngx, ngy):
+    if ngx * ngy <= 64:
+        return [[(dx, dy) for dx in range(ngx) for dy in range(ngy) if dx or dy]]
+    return [[(0, dy) for dy in range(1, ngy)], [(dx, 0) for dx in range(1, ngx)]]
+
+
 def kernel(
     ngx, ngy,
     pops, heat_level, obstacle, table,
     out_p, out_v,
-    st0, st1, rd, rho_s, v0, v1, hl, ob, solid_s, obuf, pm_src, pm_gy, pm_gx,
-    load_sem, a_send, a_recv, b_send, b_recv, p_send, p_recv, out_sem,
+    st0, st1, rd, rho_s, v0, v1, hl, ob, tb, solid_s, pm_src, *rest,
 ):
+    *pm_bufs, load_sem, a_send, a_recv, b_send, b_recv, p_send, p_recv = rest
     _, sx, sy, nz = pops.shape
     levels = table.shape[0]
     gx = lax.axis_index("gx")
@@ -80,26 +85,31 @@
     load_p.start()
     load_h.start()
     load_o.start()
+    load_t = pltpu.make_async_copy(table, tb, load_sem.at[3])
+    load_t.start()
 
     barrier = pltpu.get_barrier_semaphore()
 
     def greet(x, y):
         pl.semaphore_signal(barrier, inc=1, device_id={"gx": x, "gy": y}, device_id_type=pl.DeviceIdType.MESH)
 
-    for d in range(1, ngx):
-        greet(lax.rem(gx + d, ngx), gy)
-    for d in range(1, ngy):
-        greet(gx, lax.rem(gy + d, ngy))
-
-    @pl.when(has_up)
-    def _():
-        greet(right, gy + 1)
-        greet(left, gy + 1)
-
-    @pl.when(has_down)
-    def _():
-        greet(right, gy - 1)
-        greet(left, gy - 1)
+    groups = peak_groups(ngx, ngy)
+    partners = sum(len(group) for group in groups)
+    for group in groups:
+        for dx, dy in group:
+            greet(lax.rem(gx + dx, ngx), lax.rem(gy + dy, ngy))
+    if len(groups) > 1:
+        partners = partners + 2 * (jnp.where(has_up, 1, 0) + jnp.where(has_down, 1, 0))
+
+        @pl.when(has_up)
+        def _():
+            greet(right, gy + 1)
+            greet(left, gy + 1)
+
+        @pl.when(has_down)
+        def _():
+            greet(right, gy - 1)
+            greet(left, gy - 1)
 
     def zero_rim(rows):
         for ref in (st0, st1, v0, v1):
@@ -179,11 +189,13 @@
 
         return wait_recv, wait_send
 
-    def spread(step, phase, value, buf):
-        count = buf.shape[1]
+    def spread(step, phase, value):
+        group = peak_groups(ngx, ngy)[phase]
+        count = len(group)
+        buf = pm_bufs[phase]
         pm_src[step, phase] = value
-        for d in range(1, count + 1):
-            place = {"gy": lax.rem(gy + d, ngy)} if phase == 0 else {"gx": lax.rem(gx + d, ngx)}
+        for d, (dx, dy) in enumerate(group, 1):
+            place = {"gx": lax.rem(gx + dx, ngx), "gy": lax.rem(gy + dy, ngy)}
             pltpu.make_async_remote_copy(
                 src_ref=pm_src.at[step, phase],
                 dst_ref=buf.at[step, d - 1],
@@ -287,19 +299,19 @@
 
     gone = []
 
-    partners = (ngx - 1) + (ngy - 1) + 2 * (jnp.where(has_up, 1, 0) + jnp.where(has_down, 1, 0))
     load_p.wait()
     pl.semaphore_wait(barrier, partners)
     wait_a, sent = exchange(st0, a_send.at[0], a_recv.at[0], 8, moving)
     gone.append(sent)
     load_h.wait()
     load_o.wait()
+    load_t.wait()
     for x, r in blocks:
         rows = pl.ds(r, ROW)
         code = hl[x, rows, :]
         heat = jnp.zeros((ROW, nz), jnp.float32)
         for level in range(levels):
-            heat = jnp.where(code == level, table[level], heat)
+            heat = jnp.where(code == level, tb[level], heat)
         grid_y = gy * sy + r + lax.broadcasted_iota(jnp.int32, (ROW, nz), 0)
         solid = (
             (ob[x, rows, :] == 1) | (grid_y == 0) | (grid_y == ngy * sy - 1) | first_lane | last_lane
@@ -311,11 +323,12 @@
 
     wait_b, sent = exchange(v0, b_send.at[0], b_recv.at[0], 4, lambda direction: [pl.ds(0, 4)])
     gone.append(sent)
-    wait_y, sent = spread(0, 0, peak, pm_gy)
+    wait_peak, sent = spread(0, 0, peak)
     gone.append(sent)
     wait_b()
-    wait_x, sent = spread(0, 1, wait_y(), pm_gx)
-    gone.append(sent)
+    for phase in range(1, len(pm_bufs)):
+        wait_peak, sent = spread(0, phase, wait_peak())
+        gone.append(sent)
 
     def store_st1(k, x, r, value):
         st1[k, x + 1, pl.ds(ROW + r, ROW), :] = value
@@ -324,39 +337,45 @@
 
     wait_a, sent = exchange(st1, a_send.at[1], a_recv.at[1], 8, moving)
     gone.append(sent)
-    fs = scale_of(wait_x())
+    fs = scale_of(wait_peak())
     wait_a()
     peak = streamed(st1, fs)
 
     wait_b, sent = exchange(v1, b_send.at[1], b_recv.at[1], 4, lambda direction: [pl.ds(0, 3)])
     gone.append(sent)
-    wait_y, sent = spread(1, 0, peak, pm_gy)
-    gone.append(sent)
-    send_v = pltpu.make_async_copy(v1.at[:, own_x, own_y, :], out_v, out_sem.at[19])
-    send_v.start()
+    wait_peak, sent = spread(1, 0, peak)
+    gone.append(sent)
+    for x, r in blocks:
+        for c in range(3):
+            out_v[c, x, pl.ds(r, ROW), :] = v1[c, x + 1, pl.ds(ROW + r, ROW), :]
     wait_b()
-    wait_x, sent = spread(1, 1, wait_y(), pm_gx)
-    gone.append(sent)
+    for phase in range(1, len(pm_bufs)):
+        wait_peak, sent = spread(1, phase, wait_peak())
+        gone.append(sent)
 
     def store_out(k, x, r, value):
-        obuf[k, x, pl.ds(r, ROW), :] = value
+        out_p[k, x, pl.ds(r, ROW), :] = value
 
     collided(v1, store_out)
-    outs = {k: pltpu.make_async_copy(obuf.at[k], out_p.at[k], out_sem.at[k]) for k in range(19)}
-    for k in FLAT:
-        outs[k].start()
-    fs = scale_of(wait_x())
+    fs = scale_of(wait_peak())
     lift = {(x, r): fs * v0[3, x + 1, pl.ds(ROW + r, ROW), :] for x, r in blocks}
     for k in LIFTED:
         for x, r in blocks:
             rows = pl.ds(r, ROW)
-            obuf[k, x, rows, :] = obuf[k, x, rows, :] + (3.0 * WEIGHT[k] * CS[k][2]) * lift[(x, r)]
-        outs[k].start()
+            out_p[k, x, rows, :] = out_p[k, x, rows, :] + (3.0 * WEIGHT[k] * CS[k][2]) * lift[(x, r)]
     for sent in gone:
         sent()
-    send_v.wait()
-    for k in range(19):
-        outs[k].wait()
+
+
+def write_out(pops, vel, out_p, out_v, sems):
+    copies = [
+        pltpu.make_async_copy(pops, out_p, sems.at[0]),
+        pltpu.make_async_copy(vel, out_v, sems.at[1]),
+    ]
+    for copy in copies:
+        copy.start()
+    for copy in copies:
+        copy.wait()
 
 
 def local(populations, heat_level, obstacle, heat_table):
@@ -366,14 +385,19 @@
     f32 = jnp.float32
     wide = (sx + 2, sy + 2 * ROW, nz)
     dma = pltpu.SemaphoreType.DMA
-    return pl.pallas_call(
+    groups = peak_groups(ngx, ngy)
+    phases = len(groups)
+    vmem = pl.BlockSpec(memory_space=pltpu.VMEM)
+    anywhere = pl.BlockSpec(memory_space=pltpu.HBM)
+    shapes = (
+        jax.ShapeDtypeStruct(populations.shape, f32),
+        jax.ShapeDtypeStruct((3, sx, sy, nz), f32),
+    )
+    pops, velocity = pl.pallas_call(
         functools.partial(kernel, ngx, ngy),
-        out_shape=(
-            jax.ShapeDtypeStruct(populations.shape, f32),
-            jax.ShapeDtypeStruct((3, sx, sy, nz), f32),
-        ),
-        in_specs=[pl.BlockSpec(memory_space=pl.ANY)] * 3 + [pl.BlockSpec(memory_space=pltpu.SMEM)],
-        out_specs=[pl.BlockSpec(memory_space=pl.ANY)] * 2,
+        out_shape=shapes,
+        in_specs=[anywhere] * 4,
+        out_specs=[vmem] * 2,
         scratch_shapes=[
             pltpu.VMEM((19,) + wide, f32),
             pltpu.VMEM((19,) + wide, f32),
@@ -383,23 +407,32 @@
             pltpu.VMEM((3,) + wide, f32),
             pltpu.VMEM((sx, sy, nz), jnp.int32),
             pltpu.VMEM((sx, sy, nz), jnp.int32),
+            pltpu.SMEM(heat_table.shape, f32),
             pltpu.VMEM((sx, sy, nz), jnp.int32),
-            pltpu.VMEM((19, sx, sy, nz), f32),
-            pltpu.VMEM((STEPS, 2, ROW, nz), f32),
-            pltpu.VMEM((STEPS, ngy - 1, ROW, nz), f32),
-            pltpu.VMEM((STEPS, ngx - 1, ROW, nz), f32),
-            dma((3,)),
+            pltpu.VMEM((STEPS, phases, ROW, nz), f32),
+            *[pltpu.VMEM((STEPS, len(group), ROW, nz), f32) for group in groups],
+            dma((4,)),
             dma((STEPS, 8)),
             dma((STEPS, 8)),
             dma((STEPS, 4)),
             dma((STEPS, 4)),
-            dma((STEPS, 2)),
-            dma((STEPS, 2)),
-            dma((20,)),
+            dma((STEPS, phases)),
+            dma((STEPS, phases)),
         ],
-        compiler_params=pltpu.CompilerParams(collective_id=0, has_side_effects=True),
+        compiler_params=pltpu.CompilerParams(
+            collective_id=0, has_side_effects=True, vmem_limit_bytes=24 * 1024 * 1024
+        ),
         name="lattice_steps",
     )(populations, heat_level, obstacle, heat_table)
+    return pl.pallas_call(
+        write_out,
+        out_shape=shapes,
+        in_specs=[vmem] * 2,
+        out_specs=[anywhere] * 2,
+        scratch_shapes=[dma((2,))],
+        compiler_params=pltpu.CompilerParams(vmem_limit_bytes=8 * 1024 * 1024),
+        name="write_out",
+    )(pops, velocity)
 
 
 def solution(mesh):

time: 31.7 us -> 30.5 us (0.962)
  Pallas kernels: 28.3 us -> 26.3 us
  local copies, waits for them, and re-layouts: 2.63 us -> 3.24 us
    pallas_call x1 -> x2, Pallas kernels: 28.3 us -> 26.3 us  [the longest x1 25.5 us: local(): pl.pallas_call(functools.partial(kernel, ngx, ngy), out_shape=shapes, in_...]
    unnamed x4 -> x8, local copies, waits for them, and re-layouts: 2.63 us -> 3.24 us
where the time goes in v2:
time: 30.5 us; the launch traced here: 30.2 us
  Pallas kernels  26.3 us (86%)
  local copies, waits for them, and re-layouts  3.24 us (11%)
  between operations  0.65 us (2%)
    pallas_call x1, Pallas kernels, local(): pl.pallas_call(functools.partial(kernel, ngx, ngy), out_shape=shapes, in_...  25.5 us
    unnamed x8, local copies, waits for them, and re-layouts  3.24 us
    pallas_call x1, Pallas kernels, local(): pl.pallas_call(write_out, out_shape=shapes, in_specs=[vmem] * 2, out_spec...  0.87 us

profile of v2, /device:TPU:0, one launch (start us, length us, event | category | flops | bytes accessed | tf_op | source)
XLA Modules:
  0.0 30.2 jit_solution(8459734587139792490)
XLA Ops:
  0.6 0.0 copy-start
  0.6 1.1 %copy-done = f32[19,4,16,128]{3,2,1,0:T(8,128)S(1)} copy-done((f32[19,4,16,128]{3,2,1,0:T(8,128)S(1)}, f32[19,4,16,128]{3,2,1,0:T(8,128)}, u32[]{:S(2)}) %copy-start) | copy-done | bytes 622616
  1.7 0.0 copy-start.1
  1.7 0.8 %copy-done.1 = s32[4,16,128]{2,1,0:T(8,128)S(1)} copy-done((s32[4,16,128]{2,1,0:T(8,128)S(1)}, s32[4,16,128]{2,1,0:T(8,128)}, u32[]{:S(2)}) %copy-start.1) | copy-done | bytes 32792
  2.5 0.0 copy-start.2
  2.5 0.8 %copy-done.2 = s32[4,16,128]{2,1,0:T(8,128)S(1)} copy-done((s32[4,16,128]{2,1,0:T(8,128)S(1)}, s32[4,16,128]{2,1,0:T(8,128)}, u32[]{:S(2)}) %copy-start.2) | copy-done | bytes 32792
  3.2 0.0 copy-start.3
  3.2 0.7 %copy-done.3 = f32[8]{0:T(128)S(1)} copy-done((f32[8]{0:T(128)S(1)}, f32[8]{0:T(128)}, u32[]{:S(2)}) %copy-start.3) | copy-done | bytes 56
  3.9 25.5 %lattice_steps.1 = (f32[19,4,16,128]{3,2,1,0:T(8,128)S(1)}, f32[3,4,16,128]{3,2,1,0:T(8,128)S(1)}) custom-call(f32[19,4,16,128]{3,2,1,0:T(8,128)S(1)} %copy-done, s32[4,16,128]{2,1,0:T(8,128)S(1)} %copy-done.1, s32[4,16,128]{2,1,0:T(8,128)S(1)} %copy-done.2, f32[8]{0:T(128)S(1)} %copy-done.3), custom_call_target="tpu_custom_call" | custom-call | tf_op jit(solution)/shard_map/lattice_steps/pallas_call | solution.py:396
  29.4 0.9 %write_out.1 = (f32[19,4,16,128]{3,2,1,0:T(8,128)}, f32[3,4,16,128]{3,2,1,0:T(8,128)}) custom-call(f32[19,4,16,128]{3,2,1,0:T(8,128)S(1)} %get-tuple-element.4.pops, f32[3,4,16,128]{3,2,1,0:T(8,128)S(1)} %get-tuple-element.5.vel), custom_call_target="tpu_custom_call" | custom-call | tf_op jit(solution)/shard_map/write_out/pallas_call | solution.py:427
Async XLA Ops:
  0.6 1.1 %copy-start = (f32[19,4,16,128]{3,2,1,0:T(8,128)S(1)}, f32[19,4,16,128]{3,2,1,0:T(8,128)}, u32[]{:S(2)}) copy-start(f32[19,4,16,128]{3,2,1,0:T(8,128)} %pops.1) | copy-start | bytes 1867780
  1.7 0.8 %copy-start.1 = (s32[4,16,128]{2,1,0:T(8,128)S(1)}, s32[4,16,128]{2,1,0:T(8,128)}, u32[]{:S(2)}) copy-start(s32[4,16,128]{2,1,0:T(8,128)} %heat_level.1) | copy-start | bytes 98308
  2.5 0.8 %copy-start.2 = (s32[4,16,128]{2,1,0:T(8,128)S(1)}, s32[4,16,128]{2,1,0:T(8,128)}, u32[]{:S(2)}) copy-start(s32[4,16,128]{2,1,0:T(8,128)} %obstacle.1) | copy-start | bytes 98308
  3.2 0.7 %copy-start.3 = (f32[8]{0:T(128)S(1)}, f32[8]{0:T(128)}, u32[]{:S(2)}) copy-start(f32[8]{0:T(128)} %table.1) | copy-start | bytes 100

commit v3 on v2

--- a/solution.py
+++ b/solution.py
@@ -423,7 +423,7 @@
             collective_id=0, has_side_effects=True, vmem_limit_bytes=24 * 1024 * 1024
         ),
         name="lattice_steps",
-    )(populations, heat_level, obstacle, heat_table)
+    )(*[pltpu.with_memory_space_constraint(a, pltpu.HBM) for a in (populations, heat_level, obstacle, heat_table)])
     return pl.pallas_call(
         write_out,
         out_shape=shapes,

time: 30.5 us -> 27 us (0.89)
  local copies, waits for them, and re-layouts: 3.24 us -> 0 us
    unnamed x8 -> x0, local copies, waits for them, and re-layouts: 3.24 us -> none
where the time goes in v3:
time: 27 us; the launch traced here: 26.9 us
  Pallas kernels  26.2 us (97%)
  between operations  0.64 us (2%)
    pallas_call x1, Pallas kernels, local(): pl.pallas_call(functools.partial(kernel, ngx, ngy), out_shape=shapes, in_...  25.4 us
    pallas_call x1, Pallas kernels, local(): pl.pallas_call(write_out, out_shape=shapes, in_specs=[vmem] * 2, out_spec...  0.87 us

profile of v3, /device:TPU:0, one launch (start us, length us, event | category | flops | bytes accessed | tf_op | source)
XLA Modules:
  0.0 26.9 jit_solution(17492955169397434608)
XLA Ops:
  0.6 25.4 %lattice_steps.1 = (f32[19,4,16,128]{3,2,1,0:T(8,128)S(1)}, f32[3,4,16,128]{3,2,1,0:T(8,128)S(1)}) custom-call(f32[19,4,16,128]{3,2,1,0:T(8,128)} %pops.1, s32[4,16,128]{2,1,0:T(8,128)} %heat_level.1, s32[4,16,128]{2,1,0:T(8,128)} %obstacle.1, f32[8]{0:T(128)} %table.1), custom_call_target="tpu_custom_call" | custom-call | tf_op jit(solution)/shard_map/lattice_steps/pallas_call | solution.py:396
  26.0 0.9 %write_out.1 = (f32[19,4,16,128]{3,2,1,0:T(8,128)}, f32[3,4,16,128]{3,2,1,0:T(8,128)}) custom-call(f32[19,4,16,128]{3,2,1,0:T(8,128)S(1)} %get-tuple-element.4.pops, f32[3,4,16,128]{3,2,1,0:T(8,128)S(1)} %get-tuple-element.5.vel), custom_call_target="tpu_custom_call" | custom-call | tf_op jit(solution)/shard_map/write_out/pallas_call | solution.py:427
